TPU v7x, 256 devices: a whole 4x4x8 slice. The times are simulated.
256 devices in a mesh: ctx: 64 (over x, z, core), head: 4 (over y).
Axes of the slice: x: 4, y: 4, z: 8, core: 2. Of those that a mesh axis runs over, the one named last changes fastest.
Arguments:
- query: bfloat16 [49152, 1024], P('ctx', 'head'), parts along dimension 1, may hold values from -6 to 6
- key_value: bfloat16 [49152, 1024], P('ctx', 'head'), parts along dimension 1, may hold values from -6 to 6
- d_out: bfloat16 [49152, 1024], P('ctx', 'head'), parts along dimension 1, may hold values from -128 to 128
- doc_starts: int32 [512], P('head'), parts along dimension 0, may hold values from 0 to 49151, as said below
Outputs:
- d_query: bfloat16 [49152, 1024], P('ctx', 'head'), parts along dimension 1
- d_key_value: bfloat16 [49152, 1024], P('ctx', 'head'), parts along dimension 1
There are 4 independent parts, one for each index of `head`. A program takes and returns all parts, laid end to end along the dimension named above; each array names one. Nothing has to cross between parts.
Inputs may be any that keep to these rules, and one draw needn't show every extreme that they name: `doc_starts`: Non-decreasing, first entry 0; the document of position p runs from the largest entry not above p up to the next larger entry or 49152; repeated entries are empty documents. A position p never belongs to a document that begins before (p // 768 - 3) * 768, and in every draw some document begins in the block of 768 positions exactly 3 blocks before the block of its last position.
All inputs are finite; a program needn't handle non-finite values.
Results may differ from a plain program's by a relative error of at most 0.0055.
Values may be sent and summed in bfloat16 or wider, within the bound.
A program may use at most 128 MiB of HBM per device.

v0:
```python
import jax
import jax.numpy as jnp
from jax import lax
from jax.sharding import PartitionSpec as P

HOPS = 3


def shifted(value, axis, steps):
    count = lax.axis_size(axis)
    first, last = (max(0, -steps), min(count, count - steps))
    return lax.ppermute(value, axis, [(source, source + steps) for source in range(first, last)])


def shards(query, key_value, d_out, doc_starts):
    tok_rows = query.shape[0]
    head_width = key_value.shape[1] // 2
    head_count = query.shape[1] // head_width
    score_scale = head_width ** (-0.5)
    shard_index = lax.axis_index("ctx")
    positions = shard_index * tok_rows + jnp.arange(tok_rows, dtype=jnp.int32)
    earlier = doc_starts[None, :] <= positions[:, None]
    owners = jnp.max(jnp.where(earlier, doc_starts[None, :], 0), axis=1)
    queries = query.reshape(tok_rows, head_count, head_width)
    grads_out = d_out.reshape(tok_rows, head_count, head_width)
    fetched = [key_value]
    for offset in range(1, HOPS + 1):
        fetched.append(shifted(key_value, "ctx", offset))

    def key_root(offset):
        return (shard_index - offset) * tok_rows

    def visible_pairs(offset):
        key_pos = key_root(offset) + jnp.arange(tok_rows, dtype=jnp.int32)
        return ((key_pos[None, :] >= owners[:, None]) & (key_pos[None, :] <= positions[:, None]))[
            None
        ]

    def scores_of(kv_block):
        return (
            jnp.einsum(
                "thd,sd->hts", queries, kv_block[:, :head_width], preferred_element_type=jnp.float32
            )
            * score_scale
        )

    def grad_prob_of(kv_block):
        return jnp.einsum(
            "thd,sd->hts", grads_out, kv_block[:, head_width:], preferred_element_type=jnp.float32
        )

    running = (
        jnp.full((head_count, tok_rows), -jnp.inf, jnp.float32),
        jnp.zeros((head_count, tok_rows), jnp.float32),
        jnp.zeros((head_count, tok_rows), jnp.float32),
    )
    for offset in range(HOPS + 1):
        absorb_kv_block = fetched[offset]
        absorb_row_top, absorb_row_total, absorb_weighted = running
        absorb_visible = visible_pairs(offset)
        absorb_scores = scores_of(absorb_kv_block)
        absorb_grad_prob = grad_prob_of(absorb_kv_block)
        block_top = jnp.max(jnp.where(absorb_visible, absorb_scores, -jnp.inf), axis=2)
        new_top = jnp.maximum(absorb_row_top, block_top)
        factor = jnp.exp(absorb_row_top - new_top)
        expos = jnp.where(absorb_visible, jnp.exp(absorb_scores - new_top[:, :, None]), 0.0)
        running = (
            new_top,
            absorb_row_total * factor + jnp.sum(expos, axis=2),
            absorb_weighted * factor + jnp.sum(expos * absorb_grad_prob, axis=2),
        )
    row_top, row_total, weighted = running
    log_total = row_top + jnp.log(row_total)
    row_delta = weighted / row_total
    query_grads = jnp.zeros((tok_rows, head_count, head_width), jnp.float32)
    shares = []
    for offset in range(HOPS + 1):
        gradients_kv_block = fetched[offset]
        visible = visible_pairs(offset)
        scores = scores_of(gradients_kv_block)
        weights = jnp.where(visible, jnp.exp(scores - log_total[:, :, None]), 0.0)
        grad_prob = grad_prob_of(gradients_kv_block)
        grad_score = (weights * (grad_prob - row_delta[:, :, None]) * score_scale).astype(
            jnp.bfloat16
        )
        low_weights = weights.astype(jnp.bfloat16)
        grad_query = jnp.einsum(
            "hts,sd->thd",
            grad_score,
            gradients_kv_block[:, :head_width],
            preferred_element_type=jnp.float32,
        )
        grad_key = jnp.einsum(
            "hts,thd->sd", grad_score, queries, preferred_element_type=jnp.float32
        )
        grad_value = jnp.einsum(
            "hts,thd->sd", low_weights, grads_out, preferred_element_type=jnp.float32
        )
        grad_query, share_grads = (
            grad_query,
            jnp.concatenate([grad_key, grad_value], axis=1).astype(jnp.bfloat16),
        )
        query_grads = query_grads + grad_query
        shares.append(share_grads)
    gathered = lax.optimization_barrier(shares[0]).astype(jnp.float32)
    for offset in range(1, HOPS + 1):
        gathered = gathered + shifted(shares[offset], "ctx", -offset).astype(jnp.float32)
    d_query = query_grads.reshape(tok_rows, head_count * head_width).astype(jnp.bfloat16)
    return (d_query, gathered.astype(jnp.bfloat16))


def solution(mesh):
    placed = (P("ctx", "head"), P("ctx", "head"), P("ctx", "head"), P("head"))
    return jax.shard_map(
        shards,
        mesh=mesh,
        in_specs=placed,
        out_specs=(P("ctx", "head"), P("ctx", "head")),
        check_vma=False,
    )
```

profile of v0, /device:TPU:23, one launch (start us, length us, event | category | flops | bytes accessed | tf_op | source)
XLA Modules:
  0.0 111.0 jit_solution(8621584942920041268)
XLA Ops:
  0.6 3.5 %collective-permute-start.1 = (bf16[768,256]{1,0:T(8,128)(2,1)}, bf16[768,256]{1,0:T(8,128)(2,1)S(1)}, u32[]{:S(2)}, u32[]{:S(2)}) collective-permute-start(bf16[768,256]{1,0:T(8,128)(2,1)} %param.5), channel_id=1, source_target_pairs={{0,8},{4,12},{8,16},{12,20},{16,24},{20,28},{24,32},{28,36},{32,40... | collective-permute-start | bytes 1179656 | tf_op jit(solution)/shard_map/ppermute | solution.py:12
  4.2 4.4 %collective-permute-start = (bf16[768,256]{1,0:T(8,128)(2,1)}, bf16[768,256]{1,0:T(8,128)(2,1)S(1)}, u32[]{:S(2)}, u32[]{:S(2)}) collective-permute-start(bf16[768,256]{1,0:T(8,128)(2,1)} %param.5), channel_id=1, source_target_pairs={{0,4},{4,8},{8,12},{12,16},{16,20},{20,24},{24,28},{28,32},{32,36}... | collective-permute-start | bytes 1179656 | tf_op jit(solution)/shard_map/ppermute | solution.py:12
  8.6 3.3 %collective-permute-start.2 = (bf16[768,256]{1,0:T(8,128)(2,1)}, bf16[768,256]{1,0:T(8,128)(2,1)}, u32[]{:S(2)}, u32[]{:S(2)}) collective-permute-start(bf16[768,256]{1,0:T(8,128)(2,1)} %param.5), channel_id=1, source_target_pairs={{0,12},{4,16},{8,20},{12,24},{16,28},{20,32},{24,36},{28,40},{32,4... | collective-permute-start | bytes 1179656 | tf_op jit(solution)/shard_map/ppermute | solution.py:12
  11.9 1.2 %copy.94 = bf16[768,256]{0,1:T(8,128)(2,1)S(1)} copy(bf16[768,256]{1,0:T(8,128)(2,1)} %param.4) | data formatting | bytes 786432 | tf_op jit(solution)/shard_map/reshape | solution.py:24
  13.1 0.0 copy-start.15
  13.1 0.0 copy-start.18
  13.1 1.3 %copy.95 = bf16[768,256]{0,1:T(8,128)(2,1)S(1)} copy(bf16[768,256]{1,0:T(8,128)(2,1)} %param.6) | data formatting | bytes 786432 | tf_op jit(solution)/shard_map/reshape | solution.py:25
  14.4 0.9 select_reduce_fusion
  15.4 2.1 %compare_and_fusion.2 = (pred[768,768]{0,1:T(8,128)(4,1)S(1)}, pred[768,768]{0,1:T(8,128)(4,1)S(1)}, pred[768,768]{0,1:T(8,128)(4,1)S(1)}, pred[768,768]{0,1:T(8,128)(4,1)S(1)}) fusion(s32[768]{0:T(1024)S(1)} %get-tuple-element.42, s32[768]{0:T(1024)S(1)} %select_reduce_fusion, s32[768]{0:T(1024)S(1)} %get-tuple-element.41, s32[768]{0:T(1024)S(1)} %get-tuple-element.40, ...), kind=kLoop, calls=%fused_computation.73 | loop fusion | flops 7077888 | bytes 2374656 | tf_op jit(solution)/shard_map/and | solution.py:35
  17.5 2.2 %fusion.31 = (f32[2,768]{1,0:T(2,128)S(1)}, f32[768,768,2]{1,0,2:T(8,128)S(1)}) fusion(pred[768,768]{0,1:T(8,128)(4,1)S(1)} %get-tuple-element.26, bf16[768,2,128]{0,2,1:T(8,128)(2,1)S(1)} %bitcast.271, bf16[768,256]{1,0:T(8,128)(2,1)} %param.5), kind=kOutput, calls=%fused_computation.51 | convolution fusion | flops 305527296 | bytes 5904384 | tf_op jit(solution)/shard_map/thd,sd->hts/dot_general | solution.py:41
  19.7 1.8 %fusion.12 = (f32[2,768]{1,0:T(2,128)S(1)}, f32[2,768]{1,0:T(2,128)S(1)}, f32[768,768,2]{1,0,2:T(8,128)S(1)}) fusion(f32[768,768,2]{1,0,2:T(8,128)S(1)} %get-tuple-element.32, f32[2,768]{1,0:T(2,128)S(1)} %get-tuple-element.31, pred[768,768]{0,1:T(8,128)(4,1)S(1)} %get-tuple-element.26, bf16[768,2,128]{0,2,1:T(8,128)(2,1)S(1)} %bitcast.262, ...), kind=kOutput, calls=%fused_computation.20 | convolution fusion | flops 309064704 | bytes 10635264 | tf_op jit(solution)/shard_map/thd,sd->hts/dot_general | solution.py:48
  21.5 1.0 fusion.26
  22.6 0.0 copy-start.16
  22.6 0.0 copy-start.9
  22.6 0.7 copy-done.9
  23.3 2.1 %fusion.21 = (f32[2,768]{1,0:T(2,128)S(1)}, f32[768,768,2]{1,0,2:T(8,128)S(1)}) fusion(pred[768,768]{0,1:T(8,128)(4,1)S(1)} %get-tuple-element.24, bf16[768,2,128]{0,2,1:T(8,128)(2,1)} %bitcast.273, bf16[768,256]{1,0:T(8,128)(2,1)} %copy-done.9), kind=kOutput, calls=%fused_computation.35 | convolution fusion | flops 305527296 | bytes 5904384 | tf_op jit(solution)/shard_map/thd,sd->hts/dot_general | solution.py:41
  25.5 2.7 %collective-permute-done.2 = bf16[768,256]{1,0:T(8,128)(2,1)} collective-permute-done((bf16[768,256]{1,0:T(8,128)(2,1)}, bf16[768,256]{1,0:T(8,128)(2,1)}, u32[]{:S(2)}, u32[]{:S(2)}) %collective-permute-start.2) | collective-permute-done | bytes 393248 | tf_op jit(solution)/shard_map/ppermute | solution.py:12
  28.1 1.9 %fusion.16 = (f32[2,768]{1,0:T(2,128)S(1)}, f32[768,768,2]{1,0,2:T(8,128)S(1)}) fusion(pred[768,768]{0,1:T(8,128)(4,1)S(1)} %get-tuple-element.25, bf16[768,2,128]{0,2,1:T(8,128)(2,1)S(1)} %bitcast.274, bf16[768,256]{1,0:T(8,128)(2,1)} %collective-permute-done.2), kind=kOutput, calls=%fused_computation.27 | convolution fusion | flops 305527296 | bytes 5904384 | tf_op jit(solution)/shard_map/thd,sd->hts/dot_general | solution.py:41
  30.1 0.0 copy-start.10
  30.1 5.1 %fusion = (f32[2,768]{1,0:T(2,128)S(1)}, f32[2,768]{1,0:T(2,128)S(1)}, f32[768,768,2]{1,0,2:T(8,128)}) fusion(f32[768,768,2]{1,0,2:T(8,128)S(1)} %get-tuple-element.28, f32[2,768]{1,0:T(2,128)S(1)} %get-tuple-element.16, pred[768,768]{0,1:T(8,128)(4,1)S(1)} %get-tuple-element.25, bf16[768,2,128]{0,2,1:T(8,128)(2,1)S(1)} %bitcast.263, ...), kind=kOutput, calls=%fused_computation.2 | convolution fusion | flops 309064704 | bytes 10635264 | tf_op jit(solution)/shard_map/thd,sd->hts/dot_general | solution.py:48
  35.3 3.8 %fusion.4 = (f32[2,768]{1,0:T(2,128)S(1)}, f32[2,768]{1,0:T(2,128)S(1)}, f32[768,768,2]{1,0,2:T(8,128)}) fusion(f32[768,768,2]{1,0,2:T(8,128)S(1)} %get-tuple-element.30, f32[2,768]{1,0:T(2,128)S(1)} %get-tuple-element.17, pred[768,768]{0,1:T(8,128)(4,1)S(1)} %get-tuple-element.24, bf16[768,2,128]{0,2,1:T(8,128)(2,1)S(1)} %bitcast.264, ...), kind=kOutput, calls=%fused_computation.8 | convolution fusion | flops 309064704 | bytes 10635264 | tf_op jit(solution)/shard_map/thd,sd->hts/dot_general | solution.py:48
  39.1 3.9 %fusion.8 = (f32[2,768]{1,0:T(2,128)S(1)}, f32[2,768]{1,0:T(2,128)S(1)}, f32[768,768,2]{1,0,2:T(8,128)}) fusion(f32[768,768,2]{1,0,2:T(8,128)S(1)} %get-tuple-element.34, f32[2,768]{1,0:T(2,128)S(1)} %get-tuple-element.18, pred[768,768]{0,1:T(8,128)(4,1)S(1)} %get-tuple-element.23, bf16[768,2,128]{0,2,1:T(8,128)(2,1)S(1)} %bitcast.265, ...), kind=kOutput, calls=%fused_computation.14 | convolution fusion | flops 309064704 | bytes 10635264 | tf_op jit(solution)/shard_map/thd,sd->hts/dot_general | solution.py:48
  43.0 2.0 %fusion.83 = bf16[768,128]{0,1:T(8,128)(2,1)} fusion(bf16[768,2,128]{0,2,1:T(8,128)(2,1)S(1)} %bitcast.266, f32[768,768,2]{1,0,2:T(8,128)S(1)} %get-tuple-element.32, f32[2,768]{1,0:T(2,128)S(1)} %get-tuple-element.14, pred[768,768]{0,1:T(8,128)(4,1)S(1)} %get-tuple-element.26), kind=kOutput, calls=%fused_computation.95 | convolution fusion | flops 306806784 | bytes 5904384 | tf_op jit(solution)/shard_map/hts,thd->sd/dot_general | solution.py:96
  45.1 2.2 %fusion.80 = bf16[768,128]{0,1:T(8,128)(2,1)} fusion(bf16[768,2,128]{0,2,1:T(8,128)(2,1)S(1)} %bitcast.267, f32[768,768,2]{1,0,2:T(8,128)S(1)} %get-tuple-element.34, f32[2,768]{1,0:T(2,128)S(1)} %get-tuple-element.14, pred[768,768]{0,1:T(8,128)(4,1)S(1)} %get-tuple-element.23), kind=kOutput, calls=%fused_computation.94 | convolution fusion | flops 306806784 | bytes 5904384 | tf_op jit(solution)/shard_map/hts,thd->sd/dot_general | solution.py:96
  47.3 2.0 %fusion.74 = bf16[768,128]{0,1:T(8,128)(2,1)} fusion(bf16[768,2,128]{0,2,1:T(8,128)(2,1)S(1)} %bitcast.268, f32[768,768,2]{1,0,2:T(8,128)S(1)} %get-tuple-element.28, f32[2,768]{1,0:T(2,128)S(1)} %get-tuple-element.14, pred[768,768]{0,1:T(8,128)(4,1)S(1)} %get-tuple-element.25), kind=kOutput, calls=%fused_computation.92 | convolution fusion | flops 306806784 | bytes 5904384 | tf_op jit(solution)/shard_map/hts,thd->sd/dot_general | solution.py:96
  49.3 2.0 %fusion.77 = bf16[768,128]{0,1:T(8,128)(2,1)} fusion(bf16[768,2,128]{0,2,1:T(8,128)(2,1)S(1)} %bitcast.269, f32[768,768,2]{1,0,2:T(8,128)S(1)} %get-tuple-element.30, f32[2,768]{1,0:T(2,128)S(1)} %get-tuple-element.14, pred[768,768]{0,1:T(8,128)(4,1)S(1)} %get-tuple-element.24), kind=kOutput, calls=%fused_computation.93 | convolution fusion | flops 306806784 | bytes 5904384 | tf_op jit(solution)/shard_map/hts,thd->sd/dot_general | solution.py:96
  51.4 0.0 copy-start.17
  51.4 14.1 %fusion.7 = (bf16[2,768,768]{1,2,0:T(8,128)(2,1)}, bf16[2,768,768]{1,2,0:T(8,128)(2,1)}, bf16[2,768,768]{1,2,0:T(8,128)(2,1)}, bf16[2,768,768]{1,2,0:T(8,128)(2,1)}) fusion(f32[768,768,2]{1,0,2:T(8,128)} %get-tuple-element.36, f32[768,768,2]{1,0,2:T(8,128)S(1)} %get-tuple-element.30, f32[2,768]{1,0:T(2,128)S(1)} %add_divide_fusion, ...), kind=kLoop, calls=%fused_computation.11 | loop fusion | flops 33030144 | bytes 49557504 | tf_op jit(solution)/shard_map/convert_element_type | solution.py:83
  65.6 3.4 %fusion.72 = bf16[768,128]{0,1:T(8,128)(2,1)} fusion(bf16[2,768,768]{1,2,0:T(8,128)(2,1)} %get-tuple-element.19, bf16[768,2,128]{0,2,1:T(8,128)(2,1)S(1)} %bitcast.275), kind=kOutput, calls=%fused_computation.90 | convolution fusion | flops 302088192 | bytes 2949120 | tf_op jit(solution)/shard_map/hts,thd->sd/dot_general | solution.py:93
  69.0 1.6 %fusion.71 = bf16[768,128]{0,1:T(8,128)(2,1)} fusion(bf16[2,768,768]{1,2,0:T(8,128)(2,1)S(1)} %copy-done.4, bf16[768,2,128]{0,2,1:T(8,128)(2,1)S(1)} %bitcast.276), kind=kOutput, calls=%fused_computation.89 | convolution fusion | flops 302088192 | bytes 2949120 | tf_op jit(solution)/shard_map/hts,thd->sd/dot_general | solution.py:93
  70.6 1.6 %fusion.73 = bf16[768,128]{0,1:T(8,128)(2,1)} fusion(bf16[2,768,768]{1,2,0:T(8,128)(2,1)S(1)} %copy-done.3, bf16[768,2,128]{0,2,1:T(8,128)(2,1)S(1)} %bitcast.277), kind=kOutput, calls=%fused_computation.91 | convolution fusion | flops 302088192 | bytes 2949120 | tf_op jit(solution)/shard_map/hts,thd->sd/dot_general | solution.py:93
  72.2 0.5 fusion.91
  72.7 1.7 %fusion.100 = f32[2,768,128]{1,2,0:T(8,128)S(1)} fusion(bf16[2,768,768]{1,2,0:T(8,128)(2,1)S(1)} %copy-done.3, bf16[768,256]{1,0:T(8,128)(2,1)} %collective-permute-done.2), kind=kOutput, calls=%fused_computation.122 | convolution fusion | flops 301989888 | bytes 3342336 | tf_op jit(solution)/shard_map/hts,sd->thd/dot_general | solution.py:87
  74.4 0.5 convolution_add_fusion.1
  75.0 0.5 fusion.57
  75.5 0.9 copy.72
  76.5 1.0 pad_maximum_fusion.3
  77.5 11.2 %collective-permute-start.5 = (bf16[768,256]{0,1:T(8,128)(2,1)S(1)}, bf16[768,256]{0,1:T(8,128)(2,1)S(1)}, u32[]{:S(2)}, u32[]{:S(2)}) collective-permute-start(bf16[768,256]{0,1:T(8,128)(2,1)S(1)} %pad_maximum_fusion.3), channel_id=1, source_target_pairs={{12,0},{16,4},{20,8},{24,12},{28,16},{32,20},{36,24},{40,28},{44,3... | collective-permute-start | bytes 1179656 | tf_op jit(solution)/shard_map/ppermute | solution.py:12
  88.7 1.0 pad_maximum_fusion.1
  89.8 1.9 %collective-permute-start.3 = (bf16[768,256]{0,1:T(8,128)(2,1)S(1)}, bf16[768,256]{0,1:T(8,128)(2,1)S(1)}, u32[]{:S(2)}, u32[]{:S(2)}) collective-permute-start(bf16[768,256]{0,1:T(8,128)(2,1)S(1)} %pad_maximum_fusion.1), channel_id=1, source_target_pairs={{4,0},{8,4},{12,8},{16,12},{20,16},{24,20},{28,24},{32,28},{36,32}... | collective-permute-start | bytes 1179656 | tf_op jit(solution)/shard_map/ppermute | solution.py:12
  91.7 1.0 pad_maximum_fusion.2
  92.7 2.0 %collective-permute-start.4 = (bf16[768,256]{0,1:T(8,128)(2,1)S(1)}, bf16[768,256]{0,1:T(8,128)(2,1)S(1)}, u32[]{:S(2)}, u32[]{:S(2)}) collective-permute-start(bf16[768,256]{0,1:T(8,128)(2,1)S(1)} %pad_maximum_fusion.2), channel_id=1, source_target_pairs={{8,0},{12,4},{16,8},{20,12},{24,16},{28,20},{32,24},{36,28},{40,32... | collective-permute-start | bytes 1179656 | tf_op jit(solution)/shard_map/ppermute | solution.py:12
  94.8 0.9 fusion.70
  95.7 5.8 %collective-permute-done.5 = bf16[768,256]{0,1:T(8,128)(2,1)S(1)} collective-permute-done((bf16[768,256]{0,1:T(8,128)(2,1)S(1)}, bf16[768,256]{0,1:T(8,128)(2,1)S(1)}, u32[]{:S(2)}, u32[]{:S(2)}) %collective-permute-start.5) | collective-permute-done | bytes 393248 | tf_op jit(solution)/shard_map/ppermute | solution.py:12
  101.5 1.9 %collective-permute-done.3 = bf16[768,256]{0,1:T(8,128)(2,1)S(1)} collective-permute-done((bf16[768,256]{0,1:T(8,128)(2,1)S(1)}, bf16[768,256]{0,1:T(8,128)(2,1)S(1)}, u32[]{:S(2)}, u32[]{:S(2)}) %collective-permute-start.3) | collective-permute-done | bytes 393248 | tf_op jit(solution)/shard_map/ppermute | solution.py:12
  103.3 6.6 %collective-permute-done.4 = bf16[768,256]{0,1:T(8,128)(2,1)S(1)} collective-permute-done((bf16[768,256]{0,1:T(8,128)(2,1)S(1)}, bf16[768,256]{0,1:T(8,128)(2,1)S(1)}, u32[]{:S(2)}, u32[]{:S(2)}) %collective-permute-start.4) | collective-permute-done | bytes 393248 | tf_op jit(solution)/shard_map/ppermute | solution.py:12
  109.9 0.2 add_convert_fusion
  110.1 0.9 copy.73
  (43 shorter events, 0.2 us)
Async XLA Ops:
  0.6 21.9 %collective-permute-start.1 = (bf16[768,256]{1,0:T(8,128)(2,1)}, bf16[768,256]{1,0:T(8,128)(2,1)S(1)}, u32[]{:S(2)}, u32[]{:S(2)}) collective-permute-start(bf16[768,256]{1,0:T(8,128)(2,1)} %param.5), channel_id=1, source_target_pairs={{0,8},{4,12},{8,16},{12,20},{16,24},{20,28},{24,32},{28,36},{32,40... | collective-permute-start | bytes 1179656 | tf_op jit(solution)/shard_map/ppermute | solution.py:12
  4.2 17.3 %collective-permute-start = (bf16[768,256]{1,0:T(8,128)(2,1)}, bf16[768,256]{1,0:T(8,128)(2,1)S(1)}, u32[]{:S(2)}, u32[]{:S(2)}) collective-permute-start(bf16[768,256]{1,0:T(8,128)(2,1)} %param.5), channel_id=1, source_target_pairs={{0,4},{4,8},{8,12},{12,16},{16,20},{20,24},{24,28},{28,32},{32,36}... | collective-permute-start | bytes 1179656 | tf_op jit(solution)/shard_map/ppermute | solution.py:12
  8.6 19.5 %collective-permute-start.2 = (bf16[768,256]{1,0:T(8,128)(2,1)}, bf16[768,256]{1,0:T(8,128)(2,1)}, u32[]{:S(2)}, u32[]{:S(2)}) collective-permute-start(bf16[768,256]{1,0:T(8,128)(2,1)} %param.5), channel_id=1, source_target_pairs={{0,12},{4,16},{8,20},{12,24},{16,28},{20,32},{24,36},{28,40},{32,4... | collective-permute-start | bytes 1179656 | tf_op jit(solution)/shard_map/ppermute | solution.py:12
  13.1 8.5 %copy-start.15 = (bf16[768,256]{0,1:T(8,128)(2,1)}, bf16[768,256]{0,1:T(8,128)(2,1)S(1)}, u32[]{:S(2)}) copy-start(bf16[768,256]{0,1:T(8,128)(2,1)S(1)} %copy.94) | copy-start | bytes 1179652
  13.1 6.7 %copy-start.18 = (bf16[768,256]{1,0:T(8,128)(2,1)S(1)}, bf16[768,256]{1,0:T(8,128)(2,1)}, u32[]{:S(2)}) copy-start(bf16[768,256]{1,0:T(8,128)(2,1)} %param.5) | copy-start | bytes 1179652
  17.5 25.5 %copy-start.8 = (pred[768,768]{0,1:T(8,128)(4,1)}, pred[768,768]{0,1:T(8,128)(4,1)S(1)}, u32[]{:S(2)}) copy-start(pred[768,768]{0,1:T(8,128)(4,1)S(1)} %get-tuple-element.26) | copy-start | bytes 1769476
  17.5 27.6 %copy-start.5 = (pred[768,768]{0,1:T(8,128)(4,1)}, pred[768,768]{0,1:T(8,128)(4,1)S(1)}, u32[]{:S(2)}) copy-start(pred[768,768]{0,1:T(8,128)(4,1)S(1)} %get-tuple-element.23) | copy-start | bytes 1769476
  17.5 29.8 %copy-start.7 = (pred[768,768]{0,1:T(8,128)(4,1)}, pred[768,768]{0,1:T(8,128)(4,1)S(1)}, u32[]{:S(2)}) copy-start(pred[768,768]{0,1:T(8,128)(4,1)S(1)} %get-tuple-element.25) | copy-start | bytes 1769476
  17.5 31.8 %copy-start.6 = (pred[768,768]{0,1:T(8,128)(4,1)}, pred[768,768]{0,1:T(8,128)(4,1)S(1)}, u32[]{:S(2)}) copy-start(pred[768,768]{0,1:T(8,128)(4,1)S(1)} %get-tuple-element.24) | copy-start | bytes 1769476
  21.5 1.1 copy-start.12
  22.6 5.6 %copy-start.16 = (bf16[768,256]{0,1:T(8,128)(2,1)S(1)}, bf16[768,256]{0,1:T(8,128)(2,1)}, u32[]{:S(2)}) copy-start(bf16[768,256]{0,1:T(8,128)(2,1)} %copy-done.15) | copy-start | bytes 1179652
  22.6 0.7 copy-start.9
  30.1 17.2 %copy-start = (f32[768,768,2]{1,0,2:T(8,128)}, f32[768,768,2]{1,0,2:T(8,128)S(1)}, u32[]{:S(2)}) copy-start(f32[768,768,2]{1,0,2:T(8,128)S(1)} %get-tuple-element.28) | copy-start | bytes 14155780
  30.1 5.1 %copy-start.10 = (bf16[768,256]{1,0:T(8,128)(2,1)S(1)}, bf16[768,256]{1,0:T(8,128)(2,1)}, u32[]{:S(2)}) copy-start(bf16[768,256]{1,0:T(8,128)(2,1)} %copy-done.9) | copy-start | bytes 1179652
  35.3 3.8 %copy-start.13 = (bf16[768,256]{1,0:T(8,128)(2,1)S(1)}, bf16[768,256]{1,0:T(8,128)(2,1)}, u32[]{:S(2)}) copy-start(bf16[768,256]{1,0:T(8,128)(2,1)} %copy-done.12) | copy-start | bytes 1179652
  51.4 14.2 %copy-start.17 = (bf16[768,256]{0,1:T(8,128)(2,1)S(1)}, bf16[768,256]{0,1:T(8,128)(2,1)}, u32[]{:S(2)}) copy-start(bf16[768,256]{0,1:T(8,128)(2,1)} %copy-done.15) | copy-start | bytes 1179652
  65.6 3.4 %copy-start.4 = (bf16[2,768,768]{1,2,0:T(8,128)(2,1)S(1)}, bf16[2,768,768]{1,2,0:T(8,128)(2,1)}, u32[]{:S(2)}) copy-start(bf16[2,768,768]{1,2,0:T(8,128)(2,1)} %get-tuple-element.20) | copy-start | bytes 7077892
  65.6 5.0 %copy-start.3 = (bf16[2,768,768]{1,2,0:T(8,128)(2,1)S(1)}, bf16[2,768,768]{1,2,0:T(8,128)(2,1)}, u32[]{:S(2)}) copy-start(bf16[2,768,768]{1,2,0:T(8,128)(2,1)} %get-tuple-element.21) | copy-start | bytes 7077892
  69.0 3.2 %copy-start.1 = (bf16[2,768,768]{1,2,0:T(8,128)(2,1)S(1)}, bf16[2,768,768]{1,2,0:T(8,128)(2,1)}, u32[]{:S(2)}) copy-start(bf16[2,768,768]{1,2,0:T(8,128)(2,1)} %get-tuple-element.22) | copy-start | bytes 7077892
  69.0 3.2 %copy-start.19 = (bf16[768,256]{1,0:T(8,128)(2,1)S(1)}, bf16[768,256]{1,0:T(8,128)(2,1)}, u32[]{:S(2)}) copy-start(bf16[768,256]{1,0:T(8,128)(2,1)} %param.5) | copy-start | bytes 1179652
  70.6 3.9 %copy-start.14 = (bf16[768,256]{1,0:T(8,128)(2,1)S(1)}, bf16[768,256]{1,0:T(8,128)(2,1)}, u32[]{:S(2)}) copy-start(bf16[768,256]{1,0:T(8,128)(2,1)} %copy-done.12) | copy-start | bytes 1179652
  72.2 2.8 %copy-start.2 = (bf16[2,768,768]{1,2,0:T(8,128)(2,1)S(1)}, bf16[2,768,768]{1,2,0:T(8,128)(2,1)}, u32[]{:S(2)}) copy-start(bf16[2,768,768]{1,2,0:T(8,128)(2,1)} %get-tuple-element.19) | copy-start | bytes 7077892
  72.2 2.8 %copy-start.11 = (bf16[768,256]{1,0:T(8,128)(2,1)S(1)}, bf16[768,256]{1,0:T(8,128)(2,1)}, u32[]{:S(2)}) copy-start(bf16[768,256]{1,0:T(8,128)(2,1)} %copy-done.9) | copy-start | bytes 1179652
  75.5 20.1 %copy-start.20 = (bf16[768,128]{0,1:T(8,128)(2,1)S(1)}, bf16[768,128]{0,1:T(8,128)(2,1)}, u32[]{:S(2)}) copy-start(bf16[768,128]{0,1:T(8,128)(2,1)} %fusion.83) | copy-start | bytes 589828
  77.5 24.0 %collective-permute-start.5 = (bf16[768,256]{0,1:T(8,128)(2,1)S(1)}, bf16[768,256]{0,1:T(8,128)(2,1)S(1)}, u32[]{:S(2)}, u32[]{:S(2)}) collective-permute-start(bf16[768,256]{0,1:T(8,128)(2,1)S(1)} %pad_maximum_fusion.3), channel_id=1, source_target_pairs={{12,0},{16,4},{20,8},{24,12},{28,16},{32,20},{36,24},{40,28},{44,3... | collective-permute-start | bytes 1179656 | tf_op jit(solution)/shard_map/ppermute | solution.py:12
  89.8 13.6 %collective-permute-start.3 = (bf16[768,256]{0,1:T(8,128)(2,1)S(1)}, bf16[768,256]{0,1:T(8,128)(2,1)S(1)}, u32[]{:S(2)}, u32[]{:S(2)}) collective-permute-start(bf16[768,256]{0,1:T(8,128)(2,1)S(1)} %pad_maximum_fusion.1), channel_id=1, source_target_pairs={{4,0},{8,4},{12,8},{16,12},{20,16},{24,20},{28,24},{32,28},{36,32}... | collective-permute-start | bytes 1179656 | tf_op jit(solution)/shard_map/ppermute | solution.py:12
  92.7 17.2 %collective-permute-start.4 = (bf16[768,256]{0,1:T(8,128)(2,1)S(1)}, bf16[768,256]{0,1:T(8,128)(2,1)S(1)}, u32[]{:S(2)}, u32[]{:S(2)}) collective-permute-start(bf16[768,256]{0,1:T(8,128)(2,1)S(1)} %pad_maximum_fusion.2), channel_id=1, source_target_pairs={{8,0},{12,4},{16,8},{20,12},{24,16},{28,20},{32,24},{36,28},{40,32... | collective-permute-start | bytes 1179656 | tf_op jit(solution)/shard_map/ppermute | solution.py:12
where the time goes:
time: 113 us; the launch traced here: 111 us
  matrix products  41 us (36%)
  starting transfers between devices  26.3 us (23%)
  other arithmetic  20.7 us (18%)
  waiting for transfers between devices  16.9 us (15%)
  local copies, waits for them, and re-layouts  5.15 us (5%)
    ppermute x6, starting transfers between devices, shifted(): lax.ppermute(value, axis, [(source, source + steps) for source in range(f...  26.3 us
    ppermute x6, waiting for transfers between devices, shifted(): lax.ppermute(value, axis, [(source, source + steps) for source in range(f...  16.9 us
    dot_general x4, matrix products, grad_prob_of(): jnp.einsum('thd,sd->hts', grads_out, kv_block[:, head_width:], preferred_...  14.6 us
    convert_element_type x1, other arithmetic, shards(): (weights * (grad_prob - row_delta[:, :, None]) * score_scale).astype(jnp....  14.1 us
    dot_general x4, matrix products, shards(): jnp.einsum('hts,thd->sd', low_weights, grads_out, preferred_element_type=...  8.32 us
    dot_general x4, matrix products, shards(): jnp.einsum('hts,thd->sd', grad_score, queries, preferred_element_type=jnp...  7.43 us
    dot_general x4, matrix products, scores_of(): jnp.einsum('thd,sd->hts', queries, kv_block[:, :head_width], preferred_el...  7.28 us
    dot_general x4, matrix products, shards(): jnp.einsum('hts,sd->thd', grad_score, gradients_kv_block[:, :head_width],...  3.31 us
  transfers between devices with their start and end apart: 6, of which 4 were waited for; matrix products, arithmetic and copies ran while one was open for 14% of the time, Pallas kernels for 0%

commit v1 on v0

v1 whole, which is shorter than its diff:
```python
import functools

import jax
import jax.numpy as jnp
from jax import lax
from jax.experimental import pallas as pl
from jax.experimental.pallas import tpu as pltpu
from jax.sharding import PartitionSpec as P

MESH = pl.DeviceIdType.MESH
HOPS = 3
CHUNK = 256
NEG = -1e30
F32 = jnp.float32
BF16 = jnp.bfloat16


def dot(a, b):
    return lax.dot_general(a, b, (((1,), (0,)), ((), ())), preferred_element_type=F32)


def dot_t(a, b):
    return lax.dot_general(a, b, (((1,), (1,)), ((), ())), preferred_element_type=F32)


def kernel(
    n, q_hbm, kv_hbm, g_hbm, starts, dq_out, dkv_out,
    qv, gv, kb, vb, qt, gt, kt, startr, eb, gp, sbuf, mrun, trun, mblk, dblk, scl, dlt, dqt,
    own_v, own_k, shv, shk, rbv, rbk,
    load_sem, sk, sv, rk, rv, sent_v, sent_k, got_v, got_k,
):
    me = lax.axis_index("ctx")
    row = lax.axis_index("head")
    odd = lax.rem(me, 2)
    even = odd == 0
    t, d = kb.shape[1], kb.shape[2]
    heads = qt.shape[0]
    chunks = t // CHUNK
    unit = d ** (-0.5)
    to_exp2 = unit * 1.4426950408889634

    def dev(step):
        return (lax.rem(me + step + n, n), row)

    loads = [
        pltpu.make_async_copy(kv_hbm.at[:, pl.ds(0, d)], kb.at[0], load_sem.at[0]),
        pltpu.make_async_copy(q_hbm, qv, load_sem.at[1]),
        pltpu.make_async_copy(kv_hbm.at[:, pl.ds(d, d)], vb.at[0], load_sem.at[2]),
        pltpu.make_async_copy(g_hbm, gv, load_sem.at[3]),
    ]
    for load in loads:
        load.start()

    barrier = pltpu.get_barrier_semaphore()

    def greet(steps):
        for step in steps:
            pl.semaphore_signal(barrier, inc=1, device_id=dev(step), device_id_type=MESH)
        pl.semaphore_wait(barrier, len(steps))

    @pl.when(even)
    def _():
        greet((1, -1, 2, -2, 3))

    @pl.when(odd == 1)
    def _():
        greet((1, -1, -3))

    def forward(buf, send, recv, which, source, slot, step):
        return pltpu.make_async_remote_copy(
            src_ref=buf.at[source], dst_ref=buf.at[slot],
            send_sem=send.at[which], recv_sem=recv.at[slot],
            device_id=dev(step), device_id_type=MESH,
        )

    def to_link(buf, send, recv):
        return forward(buf, send, recv, 0, 0, 3 - 2 * odd, 3 - 2 * odd)

    def to_partner(buf, send, recv):
        return forward(buf, send, recv, 1, 0, 1, 1)

    def relay_partner(buf, send, recv):
        return forward(buf, send, recv, 2, 1 + 2 * odd, 2, 1 - 2 * odd)

    def relay_link(buf, send, recv):
        return forward(buf, send, recv, 3, 1, 3, 2)

    loads[0].wait()
    to_link(kb, sk, rk).start()

    @pl.when(even)
    def _():
        to_partner(kb, sk, rk).start()

    loads[1].wait()
    for h in range(heads):
        qt[h] = qv[:, h * d:(h + 1) * d].T
    kt[0] = kb[0].T

    positions = me * t + lax.broadcasted_iota(jnp.int32, (1, t), 1)

    def latest(index, best):
        start = starts[index]
        return jnp.maximum(best, jnp.where(start <= positions, start, 0))

    startr[...] = lax.fori_loop(0, starts.shape[0], latest, jnp.zeros((1, t), jnp.int32))

    def scores(b, own):
        for h in range(heads):
            for c in range(chunks):
                lanes = slice(c * CHUNK, (c + 1) * CHUNK)
                rows = (c + 1) * CHUNK if own else t
                slot = (h * chunks + c) % 2
                s = dot(kb[b, :rows, :], qt[h, :, lanes]) * to_exp2
                j = lax.broadcasted_iota(jnp.int32, (rows, CHUNK), 0)
                visible = j >= startr[:, lanes] - (me - b) * t
                if own:
                    p = lax.broadcasted_iota(jnp.int32, (rows, CHUNK), 1) + c * CHUNK
                    visible = visible & (j <= p)
                s = jnp.where(visible, s, NEG)
                sbuf[slot, :rows, :] = s
                top = jnp.max(s, axis=0, keepdims=True)
                if not own:
                    before = mrun[h:h + 1, lanes]
                    top = jnp.maximum(before, top)
                e = jnp.exp2(sbuf[slot, :rows, :] - top)
                total = jnp.sum(e, axis=0, keepdims=True)
                if not own:
                    total = total + trun[h:h + 1, lanes] * jnp.exp2(before - top)
                eb[b, h, :rows, lanes] = e.astype(BF16)
                if rows < t:
                    eb[b, h, rows:, lanes] = jnp.zeros((t - rows, CHUNK), BF16)
                mrun[h:h + 1, lanes] = top
                mblk[b, h:h + 1, lanes] = top
                trun[h:h + 1, lanes] = total

    def grad_probs(b, own):
        for h in range(heads):
            for c in range(chunks):
                lanes = slice(c * CHUNK, (c + 1) * CHUNK)
                rows = (c + 1) * CHUNK if own else t
                x = dot(vb[b, :rows, :], gt[h, :, lanes])
                gp[b, h, :rows, lanes] = x
                dblk[b, h:h + 1, lanes] = jnp.sum(
                    eb[b, h, :rows, lanes].astype(F32) * x, axis=0, keepdims=True
                )

    def grad_scores(b, own):
        for h in range(heads):
            for c in range(chunks):
                lanes = slice(c * CHUNK, (c + 1) * CHUNK)
                rows = (c + 1) * CHUNK if own else t
                eb[b, h, :rows, lanes] = (
                    eb[b, h, :rows, lanes].astype(F32) * (gp[b, h, :rows, lanes] - dlt[h:h + 1, lanes])
                ).astype(BF16)

    def contract(b, rights, factor):
        total = None
        for h in range(heads):
            right = (rights[h].astype(F32) * (scl[b, h:h + 1, :] * factor)).astype(BF16)
            term = dot_t(eb[b, h], right)
            total = term if total is None else total + term
        return total

    def grad_query(b, first):
        for h in range(heads):
            for c in range(chunks):
                lanes = slice(c * CHUNK, (c + 1) * CHUNK)
                x = dot(kt[b], eb[b, h, :, lanes]) * (scl[b, h:h + 1, lanes] * unit)
                dqt[h, :, lanes] = x if first else dqt[h, :, lanes] + x

    scores(0, True)
    loads[2].wait()
    loads[3].wait()
    for h in range(heads):
        gt[h] = gv[:, h * d:(h + 1) * d].T
    grad_probs(0, True)

    def arrive(step):
        return jnp.where(jnp.logical_and(odd == 1, step > 1), 5 - step, step)

    def await_block(buf, send, recv, b):
        forward(buf, send, recv, 0, 0, b, 1).wait_recv()

    def k_step(step, carry):
        b = arrive(step)
        await_block(kb, sk, rk, b)

        @pl.when(jnp.logical_and(even, step == 1))
        def _():
            relay_link(kb, sk, rk).start()
            relay_partner(kb, sk, rk).start()
            to_link(vb, sv, rv).start()
            to_partner(vb, sv, rv).start()

        @pl.when(jnp.logical_and(odd == 1, step == 2))
        def _():
            relay_partner(kb, sk, rk).start()
            to_link(vb, sv, rv).start()

        scores(b, False)
        kt[b] = kb[b].T
        return carry

    lax.fori_loop(1, HOPS + 1, k_step, 0)

    for h in range(heads):
        inverse = 1.0 / trun[h:h + 1, :]
        for b in range(HOPS + 1):
            scl[b, h:h + 1, :] = jnp.exp2(mblk[b, h:h + 1, :] - mrun[h:h + 1, :]) * inverse

    def off_of(step):
        on_odd = jnp.where(step == 2, 3, 2 - step)
        return jnp.where(even, 3 - step, on_odd)

    def back(send_buf, land, send, recv, off):
        step = jnp.where(even, jnp.where(off == 1, -1, jnp.where(off == 2, 1, -2)), jnp.where(off == 3, -3, -1))
        slot = jnp.where(off == 1, 2, jnp.where(off == 2, 0, jnp.where(even, 1, 3)))
        return pltpu.make_async_remote_copy(
            src_ref=send_buf.at[off], dst_ref=land.at[slot],
            send_sem=send.at[off], recv_sem=recv.at[slot],
            device_id=dev(step), device_id_type=MESH,
        )

    def landed(send_buf, land, send, recv, slot):
        pltpu.make_async_remote_copy(
            src_ref=land.at[slot], dst_ref=land.at[slot],
            send_sem=send.at[0], recv_sem=recv.at[slot],
            device_id=dev(1), device_id_type=MESH,
        ).wait_recv()

    sides = {"v": (shv, rbv, sent_v, got_v), "k": (shk, rbk, sent_k, got_k)}

    def share_step(side, rights, factor):
        send_buf, land, send, recv = sides[side]

        def run(step, carry):
            off = off_of(step)
            if side == "k":
                grad_scores(off, False)
            send_buf[off] = contract(off, rights, factor).astype(BF16)

            @pl.when(step < 2)
            def _():
                back(send_buf, land, send, recv, off).start()

            return carry

        lax.fori_loop(0, HOPS, run, 0)

        @pl.when(odd == 1)
        def _():
            landed(*sides[side], 0)
            send_buf[3] = (send_buf[3].astype(F32) + land[0].astype(F32)).astype(BF16)
            back(*sides[side], 3).start()

    def combine_even(side):
        send_buf, land, send, recv = sides[side]

        @pl.when(even)
        def _():
            landed(*sides[side], 0)
            landed(*sides[side], 1)
            send_buf[1] = (
                send_buf[1].astype(F32) + land[0].astype(F32) + land[1].astype(F32)
            ).astype(BF16)
            back(*sides[side], 1).start()

    share_step("v", gt, 1.0)

    def v_step(step, carry):
        b = arrive(step)
        await_block(vb, sv, rv, b)

        @pl.when(jnp.logical_and(even, step == 1))
        def _():
            relay_link(vb, sv, rv).start()
            relay_partner(vb, sv, rv).start()

        @pl.when(jnp.logical_and(odd == 1, step == 2))
        def _():
            relay_partner(vb, sv, rv).start()

        grad_probs(b, False)
        return carry

    lax.fori_loop(1, HOPS + 1, v_step, 0)
    combine_even("v")

    for h in range(heads):
        delta = None
        for b in range(HOPS + 1):
            term = dblk[b, h:h + 1, :] * scl[b, h:h + 1, :]
            delta = term if delta is None else delta + term
        dlt[h:h + 1, :] = delta

    share_step("k", qt, unit)

    own_v[...] = contract(0, gt, 1.0)
    grad_scores(0, True)
    own_k[...] = contract(0, qt, unit)
    combine_even("k")

    grad_query(0, True)

    def dq_step(b, carry):
        grad_query(b, False)
        return carry

    lax.fori_loop(1, HOPS + 1, dq_step, 0)
    for h in range(heads):
        dq_out[:, h * d:(h + 1) * d] = dqt[h].T.astype(BF16)

    for side, own, column in (("v", own_v, d), ("k", own_k, 0)):
        send_buf, land, send, recv = sides[side]
        landed(*sides[side], 2)
        own[...] = own[...] + land[2].astype(F32)

        @pl.when(even)
        def _():
            landed(*sides[side], 3)
            own[...] = own[...] + land[3].astype(F32)

        dkv_out[:, column:column + d] = own[...].astype(BF16)

    for buf, send, recv in ((kb, sk, rk), (vb, sv, rv)):
        to_link(buf, send, recv).wait_send()
        relay_partner(buf, send, recv).wait_send()

        @pl.when(even)
        def _():
            to_partner(buf, send, recv).wait_send()
            relay_link(buf, send, recv).wait_send()

    for side in ("v", "k"):
        for off in range(1, HOPS + 1):
            back(*sides[side], off).wait_send()


def shards(n, query, key_value, d_out, doc_starts):
    t, width = key_value.shape
    d = width // 2
    heads = query.shape[1] // d
    blocks = HOPS + 1
    any_spec = pl.BlockSpec(memory_space=pl.ANY)
    vmem = pltpu.VMEM
    dma = pltpu.SemaphoreType.DMA
    return pl.pallas_call(
        functools.partial(kernel, n),
        out_shape=(
            jax.ShapeDtypeStruct(query.shape, BF16),
            jax.ShapeDtypeStruct(key_value.shape, BF16),
        ),
        in_specs=[any_spec, any_spec, any_spec, pl.BlockSpec(memory_space=pltpu.SMEM)],
        out_specs=(pl.BlockSpec(memory_space=vmem), pl.BlockSpec(memory_space=vmem)),
        scratch_shapes=[
            vmem((t, heads * d), BF16), vmem((t, heads * d), BF16),
            vmem((blocks, t, d), BF16), vmem((blocks, t, d), BF16),
            vmem((heads, d, t), BF16), vmem((heads, d, t), BF16), vmem((blocks, d, t), BF16),
            vmem((1, t), jnp.int32),
            vmem((blocks, heads, t, t), BF16), vmem((blocks, heads, t, t), F32),
            vmem((2, t, CHUNK), F32),
            vmem((heads, t), F32), vmem((heads, t), F32),
            vmem((blocks, heads, t), F32), vmem((blocks, heads, t), F32), vmem((blocks, heads, t), F32),
            vmem((heads, t), F32), vmem((heads, d, t), F32),
            vmem((t, d), F32), vmem((t, d), F32),
            vmem((blocks, t, d), BF16), vmem((blocks, t, d), BF16),
            vmem((blocks, t, d), BF16), vmem((blocks, t, d), BF16),
            dma((4,)), dma((4,)), dma((4,)), dma((4,)), dma((4,)),
            dma((4,)), dma((4,)), dma((4,)), dma((4,)),
        ],
        compiler_params=pltpu.CompilerParams(
            collective_id=0, has_side_effects=True, vmem_limit_bytes=60 * 1024 * 1024
        ),
    )(query, key_value, d_out, doc_starts)


def solution(mesh):
    placed = (P("ctx", "head"), P("ctx", "head"), P("ctx", "head"), P("head"))
    return jax.shard_map(
        functools.partial(shards, mesh.shape["ctx"]),
        mesh=mesh,
        in_specs=placed,
        out_specs=(P("ctx", "head"), P("ctx", "head")),
        check_vma=False,
    )
```

time: 113 us -> 49.1 us (0.43)
  the two profiles are of different devices: /device:TPU:23 before, /device:TPU:1 now
where the time goes in v1:
time: 49.1 us; the launch traced here: 49 us
  Pallas kernels  45.8 us (93%)
  local copies, waits for them, and re-layouts  2.57 us (5%)
  between operations  0.65 us (1%)
    pallas_call x1, Pallas kernels, shards(): pl.pallas_call(functools.partial(kernel, n), out_shape=(jax.ShapeDtypeStr...  45.8 us
    unnamed x4, local copies, waits for them, and re-layouts  2.57 us

profile of v1, /device:TPU:1, one launch (start us, length us, event | category | flops | bytes accessed | tf_op | source)
XLA Modules:
  0.0 49.0 jit_solution(10777668499512036636)
XLA Ops:
  0.6 45.8 %shard_map.59 = (bf16[768,256]{1,0:T(8,128)(2,1)}, bf16[768,256]{1,0:T(8,128)(2,1)}) custom-call(bf16[768,256]{1,0:T(8,128)(2,1)} %q_hbm.1, bf16[768,256]{1,0:T(8,128)(2,1)} %kv_hbm.1, bf16[768,256]{1,0:T(8,128)(2,1)} %g_hbm.1, s32[128]{0:T(128)} %starts.1), custom_call_target="tpu_custom_call" | custom-call | tf_op jit(solution)/shard_map/pallas_call | solution.py:348
  46.4 0.0 copy-start
  46.5 1.8 %copy.8 = bf16[768,256]{1,0:T(8,128)(2,1)} copy(bf16[768,256]{1,0:T(8,128)(2,1)} %get-tuple-element.4) | data formatting | bytes 786432
  48.3 0.0 copy-done
  48.3 0.7 %copy.9 = bf16[768,256]{1,0:T(8,128)(2,1)} copy(bf16[768,256]{1,0:T(8,128)(2,1)S(1)} %copy-done) | data formatting | bytes 786432
Async XLA Ops:
  46.4 1.8 %copy-start = (bf16[768,256]{1,0:T(8,128)(2,1)S(1)}, bf16[768,256]{1,0:T(8,128)(2,1)}, u32[]{:S(2)}) copy-start(bf16[768,256]{1,0:T(8,128)(2,1)} %get-tuple-element.5) | copy-start | bytes 1179652

commit v2 on v1

--- a/solution.py
+++ b/solution.py
@@ -10,6 +10,7 @@
 MESH = pl.DeviceIdType.MESH
 HOPS = 3
 CHUNK = 256
+PIECES = 3
 NEG = -1e30
 F32 = jnp.float32
 BF16 = jnp.bfloat16
@@ -24,8 +25,8 @@
 
 
 def kernel(
-    n, q_hbm, kv_hbm, g_hbm, starts, dq_out, dkv_out,
-    qv, gv, kb, vb, qt, gt, kt, startr, eb, gp, sbuf, mrun, trun, mblk, dblk, scl, dlt, dqt,
+    n, q_hbm, kv_hbm, g_hbm, starts_hbm, dq_out, dkv_out,
+    starts, qv, gv, kb, vb, qt, gt, kt, startr, eb, gp, sbuf, mrun, trun, mblk, dblk, scl, dlt, dqt,
     own_v, own_k, shv, shk, rbv, rbk,
     load_sem, sk, sv, rk, rv, sent_v, sent_k, got_v, got_k,
 ):
@@ -47,6 +48,7 @@
         pltpu.make_async_copy(q_hbm, qv, load_sem.at[1]),
         pltpu.make_async_copy(kv_hbm.at[:, pl.ds(d, d)], vb.at[0], load_sem.at[2]),
         pltpu.make_async_copy(g_hbm, gv, load_sem.at[3]),
+        pltpu.make_async_copy(starts_hbm, starts, load_sem.at[4]),
     ]
     for load in loads:
         load.start()
@@ -66,33 +68,64 @@
     def _():
         greet((1, -1, -3))
 
-    def forward(buf, send, recv, which, source, slot, step):
+    piece = t // PIECES
+    keys = (kb, sk, rk)
+    values = (vb, sv, rv)
+
+    def forward(group, which, source, slot, step, r):
+        buf, send, recv = group
+        rows = pl.ds(r * piece, piece)
         return pltpu.make_async_remote_copy(
-            src_ref=buf.at[source], dst_ref=buf.at[slot],
-            send_sem=send.at[which], recv_sem=recv.at[slot],
+            src_ref=buf.at[source, rows], dst_ref=buf.at[slot, rows],
+            send_sem=send.at[which, r], recv_sem=recv.at[slot, r],
             device_id=dev(step), device_id_type=MESH,
         )
 
-    def to_link(buf, send, recv):
-        return forward(buf, send, recv, 0, 0, 3 - 2 * odd, 3 - 2 * odd)
-
-    def to_partner(buf, send, recv):
-        return forward(buf, send, recv, 1, 0, 1, 1)
-
-    def relay_partner(buf, send, recv):
-        return forward(buf, send, recv, 2, 1 + 2 * odd, 2, 1 - 2 * odd)
-
-    def relay_link(buf, send, recv):
-        return forward(buf, send, recv, 3, 1, 3, 2)
+    def to_link(group, r):
+        return forward(group, 0, 0, 3 - 2 * odd, 3 - 2 * odd, r)
+
+    def to_partner(group, r):
+        return forward(group, 1, 0, 1, 1, r)
+
+    def relay_partner(group, r):
+        return forward(group, 2, 1 + 2 * odd, 2, 1 - 2 * odd, r)
+
+    def relay_link(group, r):
+        return forward(group, 3, 1, 3, 2, r)
+
+    def await_piece(group, slot, r):
+        forward(group, 0, 0, slot, 1, r).wait_recv()
+
+    def await_block(group, slot):
+        for r in range(PIECES):
+            await_piece(group, slot, r)
+
+    def send_own_link(group):
+        for r in range(PIECES):
+            to_link(group, r).start()
+
+    def send_own_partner(group):
+        for r in range(PIECES):
+            to_partner(group, r).start()
+
+    def pass_on_even(group, r):
+        await_piece(group, 1, r)
+        relay_link(group, r).start()
+        relay_partner(group, r).start()
+
+    def pass_on_odd(group, r):
+        await_piece(group, 3, r)
+        relay_partner(group, r).start()
 
     loads[0].wait()
-    to_link(kb, sk, rk).start()
+    send_own_link(keys)
 
     @pl.when(even)
     def _():
-        to_partner(kb, sk, rk).start()
+        send_own_partner(keys)
 
     loads[1].wait()
+    loads[4].wait()
     for h in range(heads):
         qt[h] = qv[:, h * d:(h + 1) * d].T
     kt[0] = kb[0].T
@@ -179,30 +212,35 @@
     def arrive(step):
         return jnp.where(jnp.logical_and(odd == 1, step > 1), 5 - step, step)
 
-    def await_block(buf, send, recv, b):
-        forward(buf, send, recv, 0, 0, b, 1).wait_recv()
-
     def k_step(step, carry):
         b = arrive(step)
-        await_block(kb, sk, rk, b)
 
         @pl.when(jnp.logical_and(even, step == 1))
         def _():
-            relay_link(kb, sk, rk).start()
-            relay_partner(kb, sk, rk).start()
-            to_link(vb, sv, rv).start()
-            to_partner(vb, sv, rv).start()
+            for r in range(PIECES):
+                pass_on_even(keys, r)
+            send_own_link(values)
+            send_own_partner(values)
 
         @pl.when(jnp.logical_and(odd == 1, step == 2))
         def _():
-            relay_partner(kb, sk, rk).start()
-            to_link(vb, sv, rv).start()
+            for r in range(PIECES):
+                pass_on_odd(keys, r)
+            send_own_link(values)
+
+        @pl.when(step != 1 + odd)
+        def _():
+            await_block(keys, b)
 
         scores(b, False)
         kt[b] = kb[b].T
         return carry
 
     lax.fori_loop(1, HOPS + 1, k_step, 0)
+
+    @pl.when(even)
+    def _():
+        pass_on_even(values, 0)
 
     for h in range(heads):
         inverse = 1.0 / trun[h:h + 1, :]
@@ -213,79 +251,102 @@
         on_odd = jnp.where(step == 2, 3, 2 - step)
         return jnp.where(even, 3 - step, on_odd)
 
-    def back(send_buf, land, send, recv, off):
+    sides = {"v": (shv, rbv, sent_v, got_v), "k": (shk, rbk, sent_k, got_k)}
+
+    def back(side, off, r):
+        send_buf, land, send, recv = sides[side]
         step = jnp.where(even, jnp.where(off == 1, -1, jnp.where(off == 2, 1, -2)), jnp.where(off == 3, -3, -1))
         slot = jnp.where(off == 1, 2, jnp.where(off == 2, 0, jnp.where(even, 1, 3)))
+        rows = pl.ds(r * piece, piece)
         return pltpu.make_async_remote_copy(
-            src_ref=send_buf.at[off], dst_ref=land.at[slot],
-            send_sem=send.at[off], recv_sem=recv.at[slot],
+            src_ref=send_buf.at[off, rows], dst_ref=land.at[slot, rows],
+            send_sem=send.at[off, r], recv_sem=recv.at[slot, r],
             device_id=dev(step), device_id_type=MESH,
         )
 
-    def landed(send_buf, land, send, recv, slot):
+    def send_back(side, off):
+        for r in range(PIECES):
+            back(side, off, r).start()
+
+    def landed(side, slot, r):
+        send_buf, land, send, recv = sides[side]
+        rows = pl.ds(r * piece, piece)
         pltpu.make_async_remote_copy(
-            src_ref=land.at[slot], dst_ref=land.at[slot],
-            send_sem=send.at[0], recv_sem=recv.at[slot],
+            src_ref=land.at[slot, rows], dst_ref=land.at[slot, rows],
+            send_sem=send.at[0, r], recv_sem=recv.at[slot, r],
             device_id=dev(1), device_id_type=MESH,
         ).wait_recv()
 
-    sides = {"v": (shv, rbv, sent_v, got_v), "k": (shk, rbk, sent_k, got_k)}
-
-    def share_step(side, rights, factor):
-        send_buf, land, send, recv = sides[side]
-
+    def share_step(side, rights, factor, extra):
         def run(step, carry):
             off = off_of(step)
             if side == "k":
                 grad_scores(off, False)
-            send_buf[off] = contract(off, rights, factor).astype(BF16)
+            sides[side][0][off] = contract(off, rights, factor).astype(BF16)
 
             @pl.when(step < 2)
             def _():
-                back(send_buf, land, send, recv, off).start()
+                send_back(side, off)
+
+            if extra is not None:
+                extra(step)
 
             return carry
 
         lax.fori_loop(0, HOPS, run, 0)
 
-        @pl.when(odd == 1)
-        def _():
-            landed(*sides[side], 0)
-            send_buf[3] = (send_buf[3].astype(F32) + land[0].astype(F32)).astype(BF16)
-            back(*sides[side], 3).start()
-
-    def combine_even(side):
+    def combine(side, off, slots, r):
         send_buf, land, send, recv = sides[side]
-
-        @pl.when(even)
-        def _():
-            landed(*sides[side], 0)
-            landed(*sides[side], 1)
-            send_buf[1] = (
-                send_buf[1].astype(F32) + land[0].astype(F32) + land[1].astype(F32)
-            ).astype(BF16)
-            back(*sides[side], 1).start()
-
-    share_step("v", gt, 1.0)
+        rows = slice(r * piece, (r + 1) * piece)
+        total = send_buf[off, rows].astype(F32)
+        for slot in slots:
+            landed(side, slot, r)
+            total = total + land[slot, rows].astype(F32)
+        send_buf[off, rows] = total.astype(BF16)
+        back(side, off, r).start()
+
+    def combine_odd(side, r):
+        combine(side, 3, (0,), r)
+
+    def combine_even(side, r):
+        combine(side, 1, (0, 1), r)
+
+    def relay_second(step):
+        @pl.when(jnp.logical_and(even, step == 1))
+        def _():
+            pass_on_even(values, 1)
+
+    share_step("v", gt, 1.0, relay_second)
+    own_v[...] = contract(0, gt, 1.0)
 
     def v_step(step, carry):
         b = arrive(step)
-        await_block(vb, sv, rv, b)
 
         @pl.when(jnp.logical_and(even, step == 1))
         def _():
-            relay_link(vb, sv, rv).start()
-            relay_partner(vb, sv, rv).start()
+            pass_on_even(values, 2)
 
         @pl.when(jnp.logical_and(odd == 1, step == 2))
         def _():
-            relay_partner(vb, sv, rv).start()
+            pass_on_odd(values, 0)
+            pass_on_odd(values, 1)
+            for r in range(PIECES):
+                combine_odd("v", r)
+            pass_on_odd(values, 2)
+
+        @pl.when(jnp.logical_and(even, step == 3))
+        def _():
+            for r in range(PIECES):
+                combine_even("v", r)
+
+        @pl.when(step != 1 + odd)
+        def _():
+            await_block(values, b)
 
         grad_probs(b, False)
         return carry
 
     lax.fori_loop(1, HOPS + 1, v_step, 0)
-    combine_even("v")
 
     for h in range(heads):
         delta = None
@@ -294,47 +355,53 @@
             delta = term if delta is None else delta + term
         dlt[h:h + 1, :] = delta
 
-    share_step("k", qt, unit)
-
-    own_v[...] = contract(0, gt, 1.0)
+    share_step("k", qt, unit, None)
+
+    @pl.when(odd == 1)
+    def _():
+        for r in range(PIECES):
+            combine_odd("k", r)
+
     grad_scores(0, True)
     own_k[...] = contract(0, qt, unit)
-    combine_even("k")
-
-    grad_query(0, True)
-
-    def dq_step(b, carry):
-        grad_query(b, False)
-        return carry
-
-    lax.fori_loop(1, HOPS + 1, dq_step, 0)
+
+    for b in range(HOPS + 1):
+        @pl.when(jnp.logical_and(even, b < PIECES))
+        def _():
+            combine_even("k", min(b, PIECES - 1))
+
+        grad_query(b, b == 0)
+
     for h in range(heads):
         dq_out[:, h * d:(h + 1) * d] = dqt[h].T.astype(BF16)
 
     for side, own, column in (("v", own_v, d), ("k", own_k, 0)):
-        send_buf, land, send, recv = sides[side]
-        landed(*sides[side], 2)
+        land = sides[side][1]
+        for r in range(PIECES):
+            landed(side, 2, r)
         own[...] = own[...] + land[2].astype(F32)
 
         @pl.when(even)
         def _():
-            landed(*sides[side], 3)
+            for r in range(PIECES):
+                landed(side, 3, r)
             own[...] = own[...] + land[3].astype(F32)
 
         dkv_out[:, column:column + d] = own[...].astype(BF16)
 
-    for buf, send, recv in ((kb, sk, rk), (vb, sv, rv)):
-        to_link(buf, send, recv).wait_send()
-        relay_partner(buf, send, recv).wait_send()
-
-        @pl.when(even)
-        def _():
-            to_partner(buf, send, recv).wait_send()
-            relay_link(buf, send, recv).wait_send()
-
-    for side in ("v", "k"):
-        for off in range(1, HOPS + 1):
-            back(*sides[side], off).wait_send()
+    for r in range(PIECES):
+        for group in (keys, values):
+            to_link(group, r).wait_send()
+            relay_partner(group, r).wait_send()
+
+            @pl.when(even)
+            def _():
+                to_partner(group, r).wait_send()
+                relay_link(group, r).wait_send()
+
+        for side in ("v", "k"):
+            for off in range(1, HOPS + 1):
+                back(side, off, r).wait_send()
 
 
 def shards(n, query, key_value, d_out, doc_starts):
@@ -342,7 +409,7 @@
     d = width // 2
     heads = query.shape[1] // d
     blocks = HOPS + 1
-    any_spec = pl.BlockSpec(memory_space=pl.ANY)
+    hbm = pl.BlockSpec(memory_space=pltpu.HBM)
     vmem = pltpu.VMEM
     dma = pltpu.SemaphoreType.DMA
     return pl.pallas_call(
@@ -351,9 +418,10 @@
             jax.ShapeDtypeStruct(query.shape, BF16),
             jax.ShapeDtypeStruct(key_value.shape, BF16),
         ),
-        in_specs=[any_spec, any_spec, any_spec, pl.BlockSpec(memory_space=pltpu.SMEM)],
+        in_specs=[hbm, hbm, hbm, hbm],
         out_specs=(pl.BlockSpec(memory_space=vmem), pl.BlockSpec(memory_space=vmem)),
         scratch_shapes=[
+            pltpu.SMEM(doc_starts.shape, jnp.int32),
             vmem((t, heads * d), BF16), vmem((t, heads * d), BF16),
             vmem((blocks, t, d), BF16), vmem((blocks, t, d), BF16),
             vmem((heads, d, t), BF16), vmem((heads, d, t), BF16), vmem((blocks, d, t), BF16),
@@ -366,8 +434,7 @@
             vmem((t, d), F32), vmem((t, d), F32),
             vmem((blocks, t, d), BF16), vmem((blocks, t, d), BF16),
             vmem((blocks, t, d), BF16), vmem((blocks, t, d), BF16),
-            dma((4,)), dma((4,)), dma((4,)), dma((4,)), dma((4,)),
-            dma((4,)), dma((4,)), dma((4,)), dma((4,)),
+            dma((5,)), *[dma((4, PIECES)) for _ in range(8)],
         ],
         compiler_params=pltpu.CompilerParams(
             collective_id=0, has_side_effects=True, vmem_limit_bytes=60 * 1024 * 1024

time: 49.1 us -> 42.4 us (0.86)
  Pallas kernels: 45.8 us -> 39.1 us
    pallas_call x1, Pallas kernels: 45.8 us -> 39.1 us  [shards(): pl.pallas_call(functools.partial(kernel, n), out_shape=(jax.ShapeDtypeStr...]
where the time goes in v2:
time: 42.4 us; the launch traced here: 42.3 us
  Pallas kernels  39.1 us (92%)
  local copies, waits for them, and re-layouts  2.57 us (6%)
  between operations  0.65 us (2%)
    pallas_call x1, Pallas kernels, shards(): pl.pallas_call(functools.partial(kernel, n), out_shape=(jax.ShapeDtypeStr...  39.1 us
    unnamed x4, local copies, waits for them, and re-layouts  2.57 us

profile of v2, /device:TPU:1, one launch (start us, length us, event | category | flops | bytes accessed | tf_op | source)
XLA Modules:
  0.0 42.3 jit_solution(7526686344617006588)
XLA Ops:
  0.6 39.1 %shard_map.59 = (bf16[768,256]{1,0:T(8,128)(2,1)}, bf16[768,256]{1,0:T(8,128)(2,1)}) custom-call(bf16[768,256]{1,0:T(8,128)(2,1)} %q_hbm.1, bf16[768,256]{1,0:T(8,128)(2,1)} %kv_hbm.1, bf16[768,256]{1,0:T(8,128)(2,1)} %g_hbm.1, s32[128]{0:T(128)} %starts_hbm.1), custom_call_target="tpu_custom_call" | custom-call | tf_op jit(solution)/shard_map/pallas_call | solution.py:415
  39.8 0.0 copy-start
  39.8 1.8 %copy.8 = bf16[768,256]{1,0:T(8,128)(2,1)} copy(bf16[768,256]{1,0:T(8,128)(2,1)} %get-tuple-element.4) | data formatting | bytes 786432
  41.6 0.0 copy-done
  41.6 0.7 %copy.9 = bf16[768,256]{1,0:T(8,128)(2,1)} copy(bf16[768,256]{1,0:T(8,128)(2,1)S(1)} %copy-done) | data formatting | bytes 786432
Async XLA Ops:
  39.8 1.8 %copy-start = (bf16[768,256]{1,0:T(8,128)(2,1)S(1)}, bf16[768,256]{1,0:T(8,128)(2,1)}, u32[]{:S(2)}) copy-start(bf16[768,256]{1,0:T(8,128)(2,1)} %get-tuple-element.5) | copy-start | bytes 1179652

commit v3 on v2

--- a/solution.py
+++ b/solution.py
@@ -26,7 +26,7 @@
 
 def kernel(
     n, q_hbm, kv_hbm, g_hbm, starts_hbm, dq_out, dkv_out,
-    starts, qv, gv, kb, vb, qt, gt, kt, startr, eb, gp, sbuf, mrun, trun, mblk, dblk, scl, dlt, dqt,
+    starts, qv, gv, kb, vb, qt, gt, kt, bias, docs, eb, gp, sbuf, mrun, trun, mblk, dblk, scl, dlt, dqt,
     own_v, own_k, shv, shk, rbv, rbk,
     load_sem, sk, sv, rk, rv, sent_v, sent_k, got_v, got_k,
 ):
@@ -55,18 +55,29 @@
 
     barrier = pltpu.get_barrier_semaphore()
 
-    def greet(steps):
-        for step in steps:
+    has_prev = me >= 2
+    has_next = me < n - 2
+
+    def greet(partner, senders, receivers):
+        def hail(step):
             pl.semaphore_signal(barrier, inc=1, device_id=dev(step), device_id_type=MESH)
-        pl.semaphore_wait(barrier, len(steps))
+
+        hail(partner[0])
+
+        @pl.when(has_prev)
+        def _():
+            for step in senders:
+                hail(step)
+
+        pl.semaphore_wait(barrier, jnp.where(has_next, 1 + len(receivers), 1))
 
     @pl.when(even)
     def _():
-        greet((1, -1, 2, -2, 3))
+        greet((1,), (-1, -2), (3, 2))
 
     @pl.when(odd == 1)
     def _():
-        greet((1, -1, -3))
+        greet((-1,), (-3,), (1,))
 
     piece = t // PIECES
     keys = (kb, sk, rk)
@@ -101,21 +112,31 @@
             await_piece(group, slot, r)
 
     def send_own_link(group):
-        for r in range(PIECES):
-            to_link(group, r).start()
+        @pl.when(has_next)
+        def _():
+            for r in range(PIECES):
+                to_link(group, r).start()
 
     def send_own_partner(group):
         for r in range(PIECES):
             to_partner(group, r).start()
 
     def pass_on_even(group, r):
-        await_piece(group, 1, r)
-        relay_link(group, r).start()
-        relay_partner(group, r).start()
+        @pl.when(has_prev)
+        def _():
+            await_piece(group, 1, r)
+
+            @pl.when(has_next)
+            def _():
+                relay_link(group, r).start()
+
+            relay_partner(group, r).start()
 
     def pass_on_odd(group, r):
-        await_piece(group, 3, r)
-        relay_partner(group, r).start()
+        @pl.when(has_prev)
+        def _():
+            await_piece(group, 3, r)
+            relay_partner(group, r).start()
 
     loads[0].wait()
     send_own_link(keys)
@@ -130,13 +151,27 @@
         qt[h] = qv[:, h * d:(h + 1) * d].T
     kt[0] = kb[0].T
 
-    positions = me * t + lax.broadcasted_iota(jnp.int32, (1, t), 1)
-
-    def latest(index, best):
-        start = starts[index]
-        return jnp.maximum(best, jnp.where(start <= positions, start, 0))
-
-    startr[...] = lax.fori_loop(0, starts.shape[0], latest, jnp.zeros((1, t), jnp.int32))
+    for b in range(1, HOPS + 1):
+        @pl.when(me < b)
+        def _():
+            kb[b] = jnp.zeros((t, d), BF16)
+            vb[b] = jnp.zeros((t, d), BF16)
+
+    count = starts.shape[1]
+    first = jnp.broadcast_to(starts[...].astype(F32), (count, count))
+    lane = lax.broadcasted_iota(jnp.int32, (count, count), 1)
+    after = jnp.where(lane == count - 1, float(n * t), pltpu.roll(first, count - 1, 1))
+    first_q, after_q = first.T[:, :1], after.T[:, :1]
+    at = (me * t + lax.broadcasted_iota(jnp.int32, (count, t), 1)).astype(F32)
+    bias[...] = jnp.where((at >= first_q) & (at < after_q), 0.0, NEG).astype(BF16)
+
+    def mark_docs(b):
+        j = ((me - b) * t + lax.broadcasted_iota(jnp.int32, (t, count), 0)).astype(F32)
+        inside = (j >= first[:1]) & (j < after[:1])
+        docs[b] = jnp.where(inside | (j < 0.0), 1.0, 0.0).astype(BF16)
+
+    for b in range(HOPS + 1):
+        mark_docs(b)
 
     def scores(b, own):
         for h in range(heads):
@@ -144,13 +179,13 @@
                 lanes = slice(c * CHUNK, (c + 1) * CHUNK)
                 rows = (c + 1) * CHUNK if own else t
                 slot = (h * chunks + c) % 2
-                s = dot(kb[b, :rows, :], qt[h, :, lanes]) * to_exp2
-                j = lax.broadcasted_iota(jnp.int32, (rows, CHUNK), 0)
-                visible = j >= startr[:, lanes] - (me - b) * t
+                left = jnp.concatenate([kb[b, :rows, :], docs[b, :rows, :]], axis=1)
+                right = jnp.concatenate([qt[h, :, lanes], bias[:, lanes]], axis=0)
+                s = dot(left, right) * to_exp2
                 if own:
+                    j = lax.broadcasted_iota(jnp.int32, (rows, CHUNK), 0)
                     p = lax.broadcasted_iota(jnp.int32, (rows, CHUNK), 1) + c * CHUNK
-                    visible = visible & (j <= p)
-                s = jnp.where(visible, s, NEG)
+                    s = jnp.where(j <= p, s, NEG)
                 sbuf[slot, :rows, :] = s
                 top = jnp.max(s, axis=0, keepdims=True)
                 if not own:
@@ -228,7 +263,7 @@
                 pass_on_odd(keys, r)
             send_own_link(values)
 
-        @pl.when(step != 1 + odd)
+        @pl.when(jnp.logical_and(step != 1 + odd, me >= b))
         def _():
             await_block(keys, b)
 
@@ -284,7 +319,7 @@
                 grad_scores(off, False)
             sides[side][0][off] = contract(off, rights, factor).astype(BF16)
 
-            @pl.when(step < 2)
+            @pl.when(jnp.logical_and(step < 2, me >= off))
             def _():
                 send_back(side, off)
 
@@ -295,21 +330,37 @@
 
         lax.fori_loop(0, HOPS, run, 0)
 
-    def combine(side, off, slots, r):
+    def add_landed(side, off, slot, r):
         send_buf, land, send, recv = sides[side]
         rows = slice(r * piece, (r + 1) * piece)
-        total = send_buf[off, rows].astype(F32)
-        for slot in slots:
-            landed(side, slot, r)
-            total = total + land[slot, rows].astype(F32)
+        landed(side, slot, r)
+        total = send_buf[off, rows].astype(F32) + land[slot, rows].astype(F32)
         send_buf[off, rows] = total.astype(BF16)
-        back(side, off, r).start()
 
     def combine_odd(side, r):
-        combine(side, 3, (0,), r)
+        @pl.when(has_prev)
+        def _():
+            add_landed(side, 3, 0, r)
+            back(side, 3, r).start()
 
     def combine_even(side, r):
-        combine(side, 1, (0, 1), r)
+        send_buf, land, send, recv = sides[side]
+        rows = slice(r * piece, (r + 1) * piece)
+
+        @pl.when(jnp.logical_and(has_prev, has_next))
+        def _():
+            landed(side, 0, r)
+            landed(side, 1, r)
+            total = send_buf[1, rows].astype(F32) + land[0, rows].astype(F32)
+            send_buf[1, rows] = (total + land[1, rows].astype(F32)).astype(BF16)
+
+        @pl.when(jnp.logical_and(has_prev, jnp.logical_not(has_next)))
+        def _():
+            add_landed(side, 1, 0, r)
+
+        @pl.when(has_prev)
+        def _():
+            back(side, 1, r).start()
 
     def relay_second(step):
         @pl.when(jnp.logical_and(even, step == 1))
@@ -339,7 +390,7 @@
             for r in range(PIECES):
                 combine_even("v", r)
 
-        @pl.when(step != 1 + odd)
+        @pl.when(jnp.logical_and(step != 1 + odd, me >= b))
         def _():
             await_block(values, b)
 
@@ -377,11 +428,14 @@
 
     for side, own, column in (("v", own_v, d), ("k", own_k, 0)):
         land = sides[side][1]
-        for r in range(PIECES):
-            landed(side, 2, r)
-        own[...] = own[...] + land[2].astype(F32)
-
-        @pl.when(even)
+
+        @pl.when(jnp.logical_or(even, has_next))
+        def _():
+            for r in range(PIECES):
+                landed(side, 2, r)
+            own[...] = own[...] + land[2].astype(F32)
+
+        @pl.when(jnp.logical_and(even, has_next))
         def _():
             for r in range(PIECES):
                 landed(side, 3, r)
@@ -391,17 +445,27 @@
 
     for r in range(PIECES):
         for group in (keys, values):
-            to_link(group, r).wait_send()
-            relay_partner(group, r).wait_send()
+            @pl.when(has_next)
+            def _():
+                to_link(group, r).wait_send()
+
+            @pl.when(has_prev)
+            def _():
+                relay_partner(group, r).wait_send()
 
             @pl.when(even)
             def _():
                 to_partner(group, r).wait_send()
+
+            @pl.when(jnp.logical_and(even, jnp.logical_and(has_prev, has_next)))
+            def _():
                 relay_link(group, r).wait_send()
 
         for side in ("v", "k"):
             for off in range(1, HOPS + 1):
-                back(side, off, r).wait_send()
+                @pl.when(me >= off)
+                def _():
+                    back(side, off, r).wait_send()
 
 
 def shards(n, query, key_value, d_out, doc_starts):
@@ -421,11 +485,11 @@
         in_specs=[hbm, hbm, hbm, hbm],
         out_specs=(pl.BlockSpec(memory_space=vmem), pl.BlockSpec(memory_space=vmem)),
         scratch_shapes=[
-            pltpu.SMEM(doc_starts.shape, jnp.int32),
+            vmem((1, doc_starts.shape[0]), jnp.int32),
             vmem((t, heads * d), BF16), vmem((t, heads * d), BF16),
             vmem((blocks, t, d), BF16), vmem((blocks, t, d), BF16),
             vmem((heads, d, t), BF16), vmem((heads, d, t), BF16), vmem((blocks, d, t), BF16),
-            vmem((1, t), jnp.int32),
+            vmem((doc_starts.shape[0], t), BF16), vmem((blocks, t, doc_starts.shape[0]), BF16),
             vmem((blocks, heads, t, t), BF16), vmem((blocks, heads, t, t), F32),
             vmem((2, t, CHUNK), F32),
             vmem((heads, t), F32), vmem((heads, t), F32),
@@ -437,9 +501,9 @@
             dma((5,)), *[dma((4, PIECES)) for _ in range(8)],
         ],
         compiler_params=pltpu.CompilerParams(
-            collective_id=0, has_side_effects=True, vmem_limit_bytes=60 * 1024 * 1024
+            collective_id=0, has_side_effects=True, vmem_limit_bytes=50 * 1024 * 1024
         ),
-    )(query, key_value, d_out, doc_starts)
+    )(*[pltpu.with_memory_space_constraint(x, pltpu.HBM) for x in (query, key_value, d_out, doc_starts.reshape(1, -1))])
 
 
 def solution(mesh):

time: 42.4 us -> 37.7 us (0.89)
  the two profiles are of different devices: /device:TPU:1 before, /device:TPU:23 now
where the time goes in v3:
time: 37.7 us; the launch traced here: 37.3 us
  Pallas kernels  35.2 us (93%)
  local copies, waits for them, and re-layouts  1.49 us (4%)
  between operations  0.64 us (2%)
    pallas_call x1, Pallas kernels, shards(): pl.pallas_call(functools.partial(kernel, n), out_shape=(jax.ShapeDtypeStr...  35.2 us
    unnamed x2, local copies, waits for them, and re-layouts  1.49 us

profile of v3, /device:TPU:23, one launch (start us, length us, event | category | flops | bytes accessed | tf_op | source)
XLA Modules:
  0.0 37.3 jit_solution(15277547516531937262)
XLA Ops:
  0.6 35.2 %shard_map.59 = (bf16[768,256]{1,0:T(8,128)(2,1)S(1)}, bf16[768,256]{1,0:T(8,128)(2,1)S(1)}) custom-call(bf16[768,256]{1,0:T(8,128)(2,1)} %q_hbm.1, bf16[768,256]{1,0:T(8,128)(2,1)} %kv_hbm.1, bf16[768,256]{1,0:T(8,128)(2,1)} %g_hbm.1, s32[1,128]{1,0:T(1,128)} %bitcast.1), custom_call_target="tpu_custom_call" | custom-call | tf_op jit(solution)/shard_map/pallas_call | solution.py:479
  35.8 0.7 %copy.8 = bf16[768,256]{1,0:T(8,128)(2,1)} copy(bf16[768,256]{1,0:T(8,128)(2,1)S(1)} %get-tuple-element.4) | data formatting | bytes 786432
  36.6 0.7 %copy.9 = bf16[768,256]{1,0:T(8,128)(2,1)} copy(bf16[768,256]{1,0:T(8,128)(2,1)S(1)} %get-tuple-element.5) | data formatting | bytes 786432

commit v4 on v3

--- a/solution.py
+++ b/solution.py
@@ -11,6 +11,7 @@
 HOPS = 3
 CHUNK = 256
 PIECES = 3
+COLUMN = 16
 NEG = -1e30
 F32 = jnp.float32
 BF16 = jnp.bfloat16
@@ -55,6 +56,9 @@
 
     barrier = pltpu.get_barrier_semaphore()
 
+    first_chip = lax.rem(me, COLUMN) < 2
+    second_even = lax.rem(me, COLUMN) == 2
+    late = lax.rem(me, COLUMN) == 6
     has_prev = me >= 2
     has_next = me < n - 2
 
@@ -144,6 +148,16 @@
     @pl.when(even)
     def _():
         send_own_partner(keys)
+
+    loads[2].wait()
+
+    @pl.when(first_chip)
+    def _():
+        send_own_link(values)
+
+        @pl.when(even)
+        def _():
+            send_own_partner(values)
 
     loads[1].wait()
     loads[4].wait()
@@ -238,7 +252,6 @@
                 dqt[h, :, lanes] = x if first else dqt[h, :, lanes] + x
 
     scores(0, True)
-    loads[2].wait()
     loads[3].wait()
     for h in range(heads):
         gt[h] = gv[:, h * d:(h + 1) * d].T
@@ -254,14 +267,25 @@
         def _():
             for r in range(PIECES):
                 pass_on_even(keys, r)
-            send_own_link(values)
-            send_own_partner(values)
+
+            @pl.when(jnp.logical_not(first_chip))
+            def _():
+                send_own_link(values)
+                send_own_partner(values)
 
         @pl.when(jnp.logical_and(odd == 1, step == 2))
         def _():
             for r in range(PIECES):
                 pass_on_odd(keys, r)
-            send_own_link(values)
+
+            @pl.when(jnp.logical_not(first_chip))
+            def _():
+                send_own_link(values)
+
+        @pl.when(jnp.logical_and(second_even, step == HOPS))
+        def _():
+            for r in range(PIECES):
+                pass_on_even(values, r)
 
         @pl.when(jnp.logical_and(step != 1 + odd, me >= b))
         def _():
@@ -273,7 +297,9 @@
 
     lax.fori_loop(1, HOPS + 1, k_step, 0)
 
-    @pl.when(even)
+    usual_even = jnp.logical_and(even, jnp.logical_not(second_even))
+
+    @pl.when(usual_even)
     def _():
         pass_on_even(values, 0)
 
@@ -363,7 +389,7 @@
             back(side, 1, r).start()
 
     def relay_second(step):
-        @pl.when(jnp.logical_and(even, step == 1))
+        @pl.when(jnp.logical_and(usual_even, step == 1))
         def _():
             pass_on_even(values, 1)
 
@@ -373,7 +399,7 @@
     def v_step(step, carry):
         b = arrive(step)
 
-        @pl.when(jnp.logical_and(even, step == 1))
+        @pl.when(jnp.logical_and(usual_even, step == 1))
         def _():
             pass_on_even(values, 2)
 
@@ -385,7 +411,7 @@
                 combine_odd("v", r)
             pass_on_odd(values, 2)
 
-        @pl.when(jnp.logical_and(even, step == 3))
+        @pl.when(jnp.logical_and(jnp.logical_and(even, jnp.logical_not(late)), step == 3))
         def _():
             for r in range(PIECES):
                 combine_even("v", r)
@@ -408,20 +434,31 @@
 
     share_step("k", qt, unit, None)
 
+    @pl.when(jnp.logical_and(even, late))
+    def _():
+        for r in range(PIECES):
+            combine_even("v", r)
+
     @pl.when(odd == 1)
     def _():
         for r in range(PIECES):
             combine_odd("k", r)
 
-    grad_scores(0, True)
-    own_k[...] = contract(0, qt, unit)
-
-    for b in range(HOPS + 1):
-        @pl.when(jnp.logical_and(even, b < PIECES))
-        def _():
-            combine_even("k", min(b, PIECES - 1))
-
-        grad_query(b, b == 0)
+
+    grad_query(3, True)
+    for r in range(PIECES):
+        @pl.when(even)
+        def _():
+            combine_even("k", r)
+
+        if r == 0:
+            grad_query(2, False)
+        if r == 1:
+            grad_query(1, False)
+        if r == 2:
+            grad_scores(0, True)
+            own_k[...] = contract(0, qt, unit)
+            grad_query(0, False)
 
     for h in range(heads):
         dq_out[:, h * d:(h + 1) * d] = dqt[h].T.astype(BF16)
@@ -476,7 +513,7 @@
     hbm = pl.BlockSpec(memory_space=pltpu.HBM)
     vmem = pltpu.VMEM
     dma = pltpu.SemaphoreType.DMA
-    return pl.pallas_call(
+    made = pl.pallas_call(
         functools.partial(kernel, n),
         out_shape=(
             jax.ShapeDtypeStruct(query.shape, BF16),
@@ -504,6 +541,29 @@
             collective_id=0, has_side_effects=True, vmem_limit_bytes=50 * 1024 * 1024
         ),
     )(*[pltpu.with_memory_space_constraint(x, pltpu.HBM) for x in (query, key_value, d_out, doc_starts.reshape(1, -1))])
+    return pl.pallas_call(
+        put_out,
+        out_shape=tuple(jax.ShapeDtypeStruct(x.shape, BF16) for x in made),
+        in_specs=[pl.BlockSpec(memory_space=pl.ANY)] * 2,
+        out_specs=(hbm, hbm),
+        scratch_shapes=[dma((2, 2))],
+        compiler_params=pltpu.CompilerParams(vmem_limit_bytes=1024 * 1024),
+    )(*made)
+
+
+def put_out(dq, dkv, dq_hbm, dkv_hbm, sem):
+    half = dq.shape[0] // 2
+    copies = [
+        pltpu.make_async_copy(
+            source.at[pl.ds(part * half, half)], target.at[pl.ds(part * half, half)], sem.at[i, part]
+        )
+        for i, (source, target) in enumerate(((dq, dq_hbm), (dkv, dkv_hbm)))
+        for part in range(2)
+    ]
+    for copy in copies:
+        copy.start()
+    for copy in copies:
+        copy.wait()
 
 
 def solution(mesh):

time: 37.7 us -> 36.8 us (0.976)
  local copies, waits for them, and re-layouts: 1.49 us -> 0 us
  Pallas kernels: 35.2 us -> 36.1 us
    unnamed x2 -> x0, local copies, waits for them, and re-layouts: 1.49 us -> none
    pallas_call x0 -> x1, Pallas kernels: none -> 0.91 us  [shards(): pl.pallas_call(put_out, out_shape=tuple((jax.ShapeDtypeStruct(x.shape, BF...]
where the time goes in v4:
time: 36.8 us; the launch traced here: 36.7 us
  Pallas kernels  36.1 us (98%)
  between operations  0.64 us (2%)
    pallas_call x1, Pallas kernels, shards(): pl.pallas_call(functools.partial(kernel, n), out_shape=(jax.ShapeDtypeStr...  35.2 us
    pallas_call x1, Pallas kernels, shards(): pl.pallas_call(put_out, out_shape=tuple((jax.ShapeDtypeStruct(x.shape, BF...  0.91 us

profile of v4, /device:TPU:23, one launch (start us, length us, event | category | flops | bytes accessed | tf_op | source)
XLA Modules:
  0.0 36.7 jit_solution(3209456393205894842)
XLA Ops:
  0.6 35.2 %shard_map.59 = (bf16[768,256]{1,0:T(8,128)(2,1)S(1)}, bf16[768,256]{1,0:T(8,128)(2,1)S(1)}) custom-call(bf16[768,256]{1,0:T(8,128)(2,1)} %q_hbm.1, bf16[768,256]{1,0:T(8,128)(2,1)} %kv_hbm.1, bf16[768,256]{1,0:T(8,128)(2,1)} %g_hbm.1, s32[1,128]{1,0:T(1,128)} %bitcast.1), custom_call_target="tpu_custom_call" | custom-call | tf_op jit(solution)/shard_map/pallas_call | solution.py:516
  35.8 0.9 %shard_map.60 = (bf16[768,256]{1,0:T(8,128)(2,1)}, bf16[768,256]{1,0:T(8,128)(2,1)}) custom-call(bf16[768,256]{1,0:T(8,128)(2,1)S(1)} %get-tuple-element.4.dq, bf16[768,256]{1,0:T(8,128)(2,1)S(1)} %get-tuple-element.5.dkv), custom_call_target="tpu_custom_call" | custom-call | tf_op jit(solution)/shard_map/pallas_call | solution.py:544

commit v5 on v4

--- a/solution.py
+++ b/solution.py
@@ -227,6 +227,16 @@
                     eb[b, h, :rows, lanes].astype(F32) * x, axis=0, keepdims=True
                 )
 
+    def grad_probs_piece(b, r):
+        rows = slice(r * piece, (r + 1) * piece)
+        for h in range(heads):
+            for c in range(chunks):
+                lanes = slice(c * CHUNK, (c + 1) * CHUNK)
+                x = dot(vb[b, rows, :], gt[h, :, lanes])
+                gp[b, h, rows, lanes] = x
+                part = jnp.sum(eb[b, h, rows, lanes].astype(F32) * x, axis=0, keepdims=True)
+                dblk[b, h:h + 1, lanes] = part if r == 0 else dblk[b, h:h + 1, lanes] + part
+
     def grad_scores(b, own):
         for h in range(heads):
             for c in range(chunks):
@@ -416,11 +426,13 @@
             for r in range(PIECES):
                 combine_even("v", r)
 
-        @pl.when(jnp.logical_and(step != 1 + odd, me >= b))
-        def _():
-            await_block(values, b)
-
-        grad_probs(b, False)
+        for r in range(PIECES):
+            @pl.when(jnp.logical_and(step != 1 + odd, me >= b))
+            def _():
+                await_piece(values, b, r)
+
+            grad_probs_piece(b, r)
+
         return carry
 
     lax.fori_loop(1, HOPS + 1, v_step, 0)

time: 36.8 us -> 36.4 us (0.989)
  Pallas kernels: 36.1 us -> 35.7 us
    pallas_call x1, Pallas kernels: 35.2 us -> 34.8 us  [shards(): pl.pallas_call(functools.partial(kernel, n), out_shape=(jax.ShapeDtypeStr...]
where the time goes in v5:
time: 36.4 us; the launch traced here: 36.3 us
  Pallas kernels  35.7 us (98%)
  between operations  0.64 us (2%)
    pallas_call x1, Pallas kernels, shards(): pl.pallas_call(functools.partial(kernel, n), out_shape=(jax.ShapeDtypeStr...  34.8 us
    pallas_call x1, Pallas kernels, shards(): pl.pallas_call(put_out, out_shape=tuple((jax.ShapeDtypeStruct(x.shape, BF...  0.91 us

profile of v5, /device:TPU:23, one launch (start us, length us, event | category | flops | bytes accessed | tf_op | source)
XLA Modules:
  0.0 36.3 jit_solution(4052088716137219718)
XLA Ops:
  0.6 34.8 %shard_map.59 = (bf16[768,256]{1,0:T(8,128)(2,1)S(1)}, bf16[768,256]{1,0:T(8,128)(2,1)S(1)}) custom-call(bf16[768,256]{1,0:T(8,128)(2,1)} %q_hbm.1, bf16[768,256]{1,0:T(8,128)(2,1)} %kv_hbm.1, bf16[768,256]{1,0:T(8,128)(2,1)} %g_hbm.1, s32[1,128]{1,0:T(1,128)} %bitcast.1), custom_call_target="tpu_custom_call" | custom-call | tf_op jit(solution)/shard_map/pallas_call | solution.py:528
  35.4 0.9 %shard_map.60 = (bf16[768,256]{1,0:T(8,128)(2,1)}, bf16[768,256]{1,0:T(8,128)(2,1)}) custom-call(bf16[768,256]{1,0:T(8,128)(2,1)S(1)} %get-tuple-element.4.dq, bf16[768,256]{1,0:T(8,128)(2,1)S(1)} %get-tuple-element.5.dkv), custom_call_target="tpu_custom_call" | custom-call | tf_op jit(solution)/shard_map/pallas_call | solution.py:556
